TPU v7x, 32 devices: a whole 2x2x4 slice. The times are simulated.
32 devices in a mesh: dp: 2 (over y), expert: 16 (over z, x, core).
Axes of the slice: x: 2, y: 2, z: 4, core: 2. Of those that a mesh axis runs over, the one named last changes fastest.
Arguments:
- routed: bfloat16 [4096, 7168], P(('dp', 'expert')), may hold values from -160 to 160
- expert_ids: int32 [4096, 8], P(('dp', 'expert')), may hold values from 0 to 127, all different within a row
- norm_gain: bfloat16 [7168], replicated, may hold values from 0.099609375 to 1.8984375
- gate_weight: bfloat16 [16, 7168, 2048], P('expert', None, 'dp'), may hold values from -0.0625 to 0.0625
- up_weight: bfloat16 [16, 7168, 2048], P('expert', None, 'dp'), may hold values from -0.0625 to 0.0625
- down_weight: bfloat16 [16, 2048, 7168], P('expert', 'dp'), may hold values from -0.125 to 0.125
- old_place: int32 [16], replicated, may hold values from 0 to 127, as said below
- new_place: int32 [16], replicated, may hold values from 0 to 127, as said below
- probe_ids: int32 [1280], P(('dp', 'expert')), may hold values from 0 to 127
Outputs:
- expert_load: float32 [128], P('expert')
- expert_energy: float32 [128], P('expert')
- probe_out: bfloat16 [1280, 7168], P(('dp', 'expert'))
Inputs may be any that keep to these rules, and one draw needn't show every extreme that they name: `old_place`: 16 different experts. `new_place`: the same 16 experts as old_place, in some order.
All inputs are finite; a program needn't handle non-finite values.
Results may differ from a plain program's by a relative error of at most 0.012.
Values may be sent and summed in bfloat16 or wider, within the bound.
A program may use at most 128 MiB of HBM per device.

v0:
```python
import math

import jax
import jax.numpy as jnp
from jax import lax
from jax.sharding import PartitionSpec as P

EXP_DEV = 8
TOP = 8


epsilon = 1e-06


def flatten_blocks(array, slots):
    length = array.size // slots
    lanes = math.gcd(length, 128)
    return array.reshape(slots, length // lanes, lanes)


def relay_rows(array, sources):
    shaped = flatten_blocks(array, sources.shape[0])
    moved = lax.all_to_all(
        jnp.take(
            lax.all_to_all(shaped, "expert", split_axis=0, concat_axis=0, tiled=True),
            sources,
            axis=0,
        ),
        "expert",
        split_axis=0,
        concat_axis=0,
        tiled=True,
    )
    return moved.reshape(array.shape)


def expert_block(normed, gate_matrix, up_matrix, down_matrix):
    piece = lax.all_gather(normed, "dp", axis=0, tiled=True)
    gate_value = jnp.dot(piece, gate_matrix, preferred_element_type=jnp.float32)
    up_value = jnp.dot(piece, up_matrix, preferred_element_type=jnp.float32)
    hidden = (jax.nn.silu(gate_value) * up_value).astype(jnp.bfloat16)
    partial_sums = jnp.dot(hidden, down_matrix, preferred_element_type=jnp.float32)
    return lax.psum_scatter(
        partial_sums.astype(jnp.bfloat16), "dp", scatter_dimension=0, tiled=True
    )


def on_device(
    routed,
    expert_ids,
    norm_gain,
    gate_weight,
    up_weight,
    down_weight,
    old_place,
    new_place,
    probe_ids,
):
    slots = lax.axis_size("expert")
    experts = EXP_DEV * slots
    tokens = routed.shape[0] * lax.axis_size("dp") * slots
    features = routed.astype(jnp.float32)
    mean_square = jnp.sum(features * features, axis=1) / routed.shape[1]
    positions = jnp.arange(experts, dtype=jnp.int32)
    onehot = jnp.sum(
        (expert_ids[:, :, None] == positions[None, None, :]).astype(jnp.float32), axis=1
    )
    columns = jnp.stack([jnp.ones_like(mean_square), mean_square])
    local_stats = jnp.dot(columns, onehot, precision=lax.Precision.HIGHEST)
    totals = lax.psum(local_stats, ("dp", "expert"))
    owned = lax.dynamic_slice_in_dim(totals, lax.axis_index("expert") * EXP_DEV, EXP_DEV, 1)
    expert_load = owned[0] * experts / (tokens * TOP)
    expert_energy = owned[1] / owned[0]
    picked_rows = jnp.take(routed, probe_ids, axis=0).astype(jnp.float32)
    scale = lax.rsqrt(jnp.take(mean_square, probe_ids) + epsilon)
    normed = (picked_rows * scale[:, None] * norm_gain.astype(jnp.float32)[None, :]).astype(
        jnp.bfloat16
    )
    slot_index = jnp.arange(slots, dtype=jnp.int32)
    matches = new_place[:, None] == old_place[None, :]
    sources = jnp.sum(jnp.where(matches, slot_index[None, :], 0), axis=1)
    targets = jnp.sum(jnp.where(matches, slot_index[:, None], 0), axis=0)
    arrived = relay_rows(normed, targets)
    computed = expert_block(arrived, gate_weight[0], up_weight[0], down_weight[0])
    probe_out = relay_rows(computed, sources)
    return (expert_load, expert_energy, probe_out)


def solution(mesh):
    in_specs = (
        P(("dp", "expert"), None),
        P(("dp", "expert"), None),
        P(),
        P("expert", None, "dp"),
        P("expert", None, "dp"),
        P("expert", "dp", None),
        P(),
        P(),
        P(("dp", "expert")),
    )
    out_specs = (P("expert"), P("expert"), P(("dp", "expert"), None))
    return jax.shard_map(
        on_device, mesh=mesh, in_specs=in_specs, out_specs=out_specs, check_vma=False
    )
```

profile of v0, /device:TPU:27, one launch (start us, length us, event | category | flops | bytes accessed | tf_op | source)
XLA Modules:
  0.0 206.9 jit_solution(12077049982817701899)
XLA Ops:
  7.2 1.9 multiply_reduce_fusion
  9.2 1.1 mul.44
  10.2 1.6 mul.45
  11.8 1.7 gather_fusion
  13.6 0.8 gather_fusion.1
  14.4 0.1 mul.41
  14.5 1.8 gather.14
  16.4 0.1 broadcast_in_dim.62
  16.5 1.5 multiply_convert_fusion
  18.0 6.3 %all-to-all-start = ((bf16[16,140,128]{2,1,0:T(8,128)(2,1)}), bf16[16,140,128]{2,1,0:T(8,128)(2,1)S(1)}, u32[]{:S(2)}, u32[]{:S(2)}) async-start(bf16[16,140,128]{2,1,0:T(8,128)(2,1)} %multiply_convert_fusion), calls=%async_computation | async-start | bytes 1179648 | tf_op jit(solution)/shard_map/all_to_all | solution.py:25
  24.4 0.2 fusion.24
  24.6 13.8 %all-to-all-done = bf16[16,140,128]{2,1,0:T(8,128)(2,1)S(1)} async-done(((bf16[16,140,128]{2,1,0:T(8,128)(2,1)}), bf16[16,140,128]{2,1,0:T(8,128)(2,1)S(1)}, u32[]{:S(2)}, u32[]{:S(2)}) %all-to-all-start) | async-done | bytes 573472 | tf_op jit(solution)/shard_map/all_to_all | solution.py:25
  38.4 0.7 gather_fusion.2
  39.1 0.1 broadcast_select_fusion.1
  39.2 19.8 %all_to_all.20 = bf16[16,140,128]{2,1,0:T(8,128)(2,1)S(1)} all-to-all(bf16[16,140,128]{2,1,0:T(8,128)(2,1)S(1)} %broadcast_select_fusion.1), channel_id=1, replica_groups=mesh['dp'=2,'expert'=16] {'expert'}, dimensions={0} | all-to-all | bytes 1146880 | tf_op jit(solution)/shard_map/all_to_all | solution.py:23
  59.0 1.4 reshape.51
  60.5 23.0 %all-gather.2.cloned.1.call-done = bf16[80,7168]{1,0:T(8,128)(2,1)} async-done(((bf16[40,7168]{1,0:T(8,128)(2,1)}), bf16[80,7168]{1,0:T(8,128)(2,1)}) %all-gather.2.cloned.1.call-update) | async-done | bytes 1146896 | tf_op jit(solution)/shard_map/all_gather | solution.py:38
  83.5 8.3 %fusion.4 = f32[80,1024]{1,0:T(8,128)S(1)} fusion(bf16[80,7168]{1,0:T(8,128)(2,1)} %all-gather.2.cloned.1.call-done, bf16[1,7168,1024]{2,1,0:T(8,128)(2,1)} %param.14), kind=kOutput, calls=%fused_computation.8 | convolution fusion | flops 1174405120 | bytes 16154624 | tf_op jit(solution)/shard_map/dot_general | solution.py:39
  91.8 15.6 %fusion.6 = bf16[80,7168]{1,0:T(8,128)(2,1)} fusion(bf16[1,1024,7168]{2,1,0:T(8,128)(2,1)} %param.16, bf16[80,7168]{1,0:T(8,128)(2,1)S(1)} %copy-done.1, bf16[1,7168,1024]{2,1,0:T(8,128)(2,1)} %param.15, f32[80,1024]{1,0:T(8,128)S(1)} %fusion.4), kind=kOutput, calls=%fused_computation.10 | convolution fusion | flops 2349875200 | bytes 31981568 | tf_op jit(solution)/shard_map/dot_general | solution.py:42
  107.3 21.6 %reduce-scatter.2.cloned.1.call-done = bf16[40,7168]{1,0:T(8,128)(2,1)} async-done(((bf16[80,7168]{1,0:T(8,128)(2,1)}), bf16[40,7168]{1,0:T(8,128)(2,1)}) %reduce-scatter.2.cloned.1.call-update) | async-done | bytes 573456 | tf_op jit(solution)/shard_map/reduce_scatter | solution.py:43
  129.0 2.6 %reshape.52 = bf16[16,140,128]{2,1,0:T(8,128)(2,1)} reshape(bf16[40,7168]{1,0:T(8,128)(2,1)} %reduce-scatter.2.cloned.1.call-done) | data formatting | bytes 1146880 | tf_op jit(solution)/shard_map/reshape | solution.py:18
  131.6 6.5 %all-to-all-start.2 = ((bf16[16,140,128]{2,1,0:T(8,128)(2,1)}), bf16[16,140,128]{2,1,0:T(8,128)(2,1)S(1)}, u32[]{:S(2)}, u32[]{:S(2)}) async-start(bf16[16,140,128]{2,1,0:T(8,128)(2,1)} %reshape.52), calls=%async_computation.3 | async-start | bytes 1179648 | tf_op jit(solution)/shard_map/all_to_all | solution.py:25
  138.1 14.1 %all-to-all-done.2 = bf16[16,140,128]{2,1,0:T(8,128)(2,1)S(1)} async-done(((bf16[16,140,128]{2,1,0:T(8,128)(2,1)}), bf16[16,140,128]{2,1,0:T(8,128)(2,1)S(1)}, u32[]{:S(2)}, u32[]{:S(2)}) %all-to-all-start.2) | async-done | bytes 573472 | tf_op jit(solution)/shard_map/all_to_all | solution.py:25
  152.2 0.7 gather_fusion.3
  152.9 0.9 broadcast_select_fusion
  153.8 5.7 %all-to-all-start.3 = ((bf16[16,140,128]{2,1,0:T(8,128)(2,1)}), bf16[16,140,128]{2,1,0:T(8,128)(2,1)S(1)}, u32[]{:S(2)}, u32[]{:S(2)}) async-start(bf16[16,140,128]{2,1,0:T(8,128)(2,1)} %broadcast_select_fusion), calls=%async_computation.4 | async-start | bytes 1179648 | tf_op jit(solution)/shard_map/all_to_all | solution.py:23
  159.6 0.1 copy.14
  159.7 0.2 convert_reduce_fusion
  159.9 0.2 fusion.25
  160.0 38.0 %psum.7 = f32[2,128]{1,0:T(2,128)S(1)} all-reduce(f32[2,128]{1,0:T(2,128)S(1)} %fusion.25), channel_id=1, replica_groups=mesh['dp'=2,'expert'=16] {'dp','expert'}, use_global_device_ids=true, to_apply=%region_2.0 | all-reduce | flops 256 | bytes 2048 | tf_op jit(solution)/shard_map/psum | solution.py:70
  198.1 0.5 fusion.27
  198.6 1.4 reshape.53
  (32 shorter events, 0.4 us)
Async XLA Ops:
  7.2 2.0 copy-start.2
  9.1 2.7 %copy-start.4 = (s32[40]{0:T(128)S(1)}, s32[40]{0:T(128)}, u32[]{:S(2)}) copy-start(s32[40]{0:T(128)} %param.19) | copy-start | bytes 484
  9.1 2.7 %copy-start = (bf16[128,7168]{1,0:T(8,128)(2,1)S(1)}, bf16[128,7168]{1,0:T(8,128)(2,1)}, u32[]{:S(2)}) copy-start(bf16[128,7168]{1,0:T(8,128)(2,1)} %param.11) | copy-start | bytes 5505028
  16.3 8.0 %copy-start.5 = (s32[16]{0:T(128)S(1)}, s32[16]{0:T(128)}, u32[]{:S(2)}) copy-start(s32[16]{0:T(128)} %param.17) | copy-start | bytes 196
  16.3 8.0 %copy-start.6 = (s32[16]{0:T(128)S(1)}, s32[16]{0:T(128)}, u32[]{:S(2)}) copy-start(s32[16]{0:T(128)} %param.18) | copy-start | bytes 196
  18.0 20.4 %all-to-all-start = ((bf16[16,140,128]{2,1,0:T(8,128)(2,1)}), bf16[16,140,128]{2,1,0:T(8,128)(2,1)S(1)}, u32[]{:S(2)}, u32[]{:S(2)}) async-start(bf16[16,140,128]{2,1,0:T(8,128)(2,1)} %multiply_convert_fusion), calls=%async_computation | async-start | bytes 1179648 | tf_op jit(solution)/shard_map/all_to_all | solution.py:25
  24.3 59.2 %all-gather.2.cloned.1.call-start = ((), (), s32[]{:S(2)}) async-start(), calls=%async_computation.5 | async-start | bytes 1720320 | tf_op jit(solution)/shard_map/all_gather | solution.py:38
  60.4 68.5 %reduce-scatter.2.cloned.1.call-start = ((), (), s32[]{:S(2)}) async-start(), calls=%async_computation.6 | async-start | bytes 1720320 | tf_op jit(solution)/shard_map/reduce_scatter | solution.py:43
  83.5 8.3 %copy-start.1 = (bf16[80,7168]{1,0:T(8,128)(2,1)S(1)}, bf16[80,7168]{1,0:T(8,128)(2,1)}, u32[]{:S(2)}) copy-start(bf16[80,7168]{1,0:T(8,128)(2,1)} %all-gather.2.cloned.1.call-done) | copy-start | bytes 3440644
  131.6 20.6 %all-to-all-start.2 = ((bf16[16,140,128]{2,1,0:T(8,128)(2,1)}), bf16[16,140,128]{2,1,0:T(8,128)(2,1)S(1)}, u32[]{:S(2)}, u32[]{:S(2)}) async-start(bf16[16,140,128]{2,1,0:T(8,128)(2,1)} %reshape.52), calls=%async_computation.3 | async-start | bytes 1179648 | tf_op jit(solution)/shard_map/all_to_all | solution.py:25
  138.1 21.5 %copy-start.3 = (s32[128,8]{0,1:T(8,128)S(1)}, s32[128,8]{0,1:T(8,128)}, u32[]{:S(2)}) copy-start(s32[128,8]{0,1:T(8,128)} %param.12) | copy-start | bytes 12292
  153.8 44.8 %all-to-all-start.3 = ((bf16[16,140,128]{2,1,0:T(8,128)(2,1)}), bf16[16,140,128]{2,1,0:T(8,128)(2,1)S(1)}, u32[]{:S(2)}, u32[]{:S(2)}) async-start(bf16[16,140,128]{2,1,0:T(8,128)(2,1)} %broadcast_select_fusion), calls=%async_computation.4 | async-start | bytes 1179648 | tf_op jit(solution)/shard_map/all_to_all | solution.py:23
Sparse Core Ops, SparseCore 0:
  60.6 22.8 all-gather.1
  107.5 21.4 reduce-scatter.1
where the time goes:
time: 211 us; the launch traced here: 207 us
  waiting for transfers between devices  72.6 us (34%)
  blocking collectives  57.7 us (27%)
  matrix products  24 us (11%)
  starting transfers between devices  18.6 us (9%)
  local copies, waits for them, and re-layouts  14.3 us (7%)
  between operations  14.2 us (7%)
  other arithmetic  5.49 us (3%)
    psum x1, blocking collectives, on_device(): totals = lax.psum(local_stats, ('dp', 'expert'))  38 us
    all_to_all x2, waiting for transfers between devices, relay_rows(): lax.all_to_all(shaped, 'expert', split_axis=0, concat_axis=0, tiled=True)  27.9 us
    all_gather x1, waiting for transfers between devices, expert_block(): piece = lax.all_gather(normed, 'dp', axis=0, tiled=True)  23 us
    reduce_scatter x1, waiting for transfers between devices, expert_block(): lax.psum_scatter(partial_sums.astype(jnp.bfloat16), 'dp', scatter_dimensi...  21.6 us
    all_to_all x1, blocking collectives, relay_rows(): lax.all_to_all(jnp.take(lax.all_to_all(shaped, 'expert', split_axis=0, co...  19.8 us
    dot_general x1, matrix products, expert_block(): jnp.dot(hidden, down_matrix, preferred_element_type=jnp.float32)  15.6 us
    all_to_all x2, starting transfers between devices, relay_rows(): lax.all_to_all(shaped, 'expert', split_axis=0, concat_axis=0, tiled=True)  12.8 us
    dot_general x1, matrix products, expert_block(): gate_value = jnp.dot(piece, gate_matrix, preferred_element_type=jnp.float32)  8.25 us
  transfers between devices with their start and end apart: 5, of which 4 were waited for; matrix products, arithmetic and copies ran while one was open for 1% of the time, Pallas kernels for 0%

commit v1 on v0

v1 whole, which is shorter than its diff:
```python
import functools

import jax
import jax.numpy as jnp
from jax import lax
from jax.experimental import pallas as pl
from jax.experimental.pallas import tpu as pltpu
from jax.sharding import PartitionSpec as P

EXP_DEV = 8
LANES = 128
MESH = pl.DeviceIdType.MESH
VMEM = pl.BlockSpec(memory_space=pltpu.VMEM)
SMEM = pl.BlockSpec(memory_space=pltpu.SMEM)
epsilon = 1e-06


def piece_width(width, n):
    w = LANES * -(-width // (LANES * n))
    while width % w:
        w += LANES
    return w


def prepare_kernel(routed, ids, probe, gain, normed, stats):
    tokens, width = routed.shape
    experts = stats.shape[1]
    total = jnp.zeros((tokens, LANES), jnp.float32)
    for c in range(width // LANES):
        x = routed[:, c * LANES : (c + 1) * LANES].astype(jnp.float32)
        total = total + x * x
    mean_square = jnp.sum(total, axis=1, keepdims=True) / width
    lane = lax.broadcasted_iota(jnp.int32, (tokens, experts), 1)
    chosen = jnp.zeros((tokens, experts), jnp.float32)
    for k in range(ids.shape[1]):
        chosen = chosen + jnp.where(ids[:, k : k + 1] == lane, 1.0, 0.0)
    stats[...] = jnp.zeros_like(stats)
    stats[0:1, :] = jnp.sum(chosen, axis=0, keepdims=True)
    stats[1:2, :] = jnp.sum(chosen * mean_square, axis=0, keepdims=True)
    probes = probe.shape[0]
    row = lax.broadcasted_iota(jnp.int32, (tokens, tokens), 0)
    column = lax.broadcasted_iota(jnp.int32, (tokens, tokens), 1)
    flat = jnp.sum(jnp.where(row == column, mean_square, 0.0), axis=0, keepdims=True)
    pick = probe[...] == lax.broadcasted_iota(jnp.int32, (probes, tokens), 1)
    scale = lax.rsqrt(jnp.sum(jnp.where(pick, flat, 0.0), axis=1, keepdims=True) + epsilon)
    pick = jnp.where(pick, 1.0, 0.0).astype(jnp.bfloat16)
    step = 512 if width % 512 == 0 else LANES
    for c in range(width // step):
        cols = slice(c * step, (c + 1) * step)
        rows = jnp.dot(pick, routed[:, cols], preferred_element_type=jnp.float32)
        normed[:, cols] = (rows * scale * gain[:, cols].astype(jnp.float32)).astype(jnp.bfloat16)


def prepare(routed, expert_ids, probe_ids, norm_gain, experts):
    probes = probe_ids.shape[0]
    width = routed.shape[1]
    return pl.pallas_call(
        prepare_kernel,
        out_shape=(
            jax.ShapeDtypeStruct((probes, width), jnp.bfloat16),
            jax.ShapeDtypeStruct((8, experts), jnp.float32),
        ),
        in_specs=[VMEM] * 4,
        out_specs=(VMEM, VMEM),
        compiler_params=pltpu.CompilerParams(vmem_limit_bytes=16 << 20),
        cost_estimate=pl.CostEstimate(flops=10**8, bytes_accessed=3 << 20, transcendentals=0),
    )(routed, expert_ids, probe_ids.reshape(probes, 1), norm_gain.reshape(1, width))


def remote(src, dst, send, recv, device):
    return pltpu.make_async_remote_copy(
        src_ref=src, dst_ref=dst, send_sem=send, recv_sem=recv, device_id=device, device_id_type=MESH
    )


def greet(g, me, d, n):
    barrier = pltpu.get_barrier_semaphore()
    for k in range(1, n):
        pl.semaphore_signal(barrier, inc=1, device_id=(g, lax.rem(me + k, n)), device_id_type=MESH)
    for c in range(1, d):
        pl.semaphore_signal(barrier, inc=1, device_id=(lax.rem(g + c, d), me), device_id_type=MESH)
    pl.semaphore_wait(barrier, n - 1 + d - 1)


class Pieces:
    def __init__(self, width, n):
        self.n = n
        self.w = piece_width(width, n)
        self.count = width // self.w

    def of(self, i):
        p = (i * self.count + self.n - 1) // self.n
        return jnp.minimum(p, self.count - 1), (p < self.count) & ((p * self.n) // self.count == i)

    def cols(self, p):
        return pl.ds(pl.multiple_of(p * self.w, self.w), self.w)


def forward_kernel(d, n, source, normed, stats, x, totals, relay, outbox, st_in, st_mid, st_dp,
                   s1, r1, s2, r2, sy, ry, ss, rs, ssy, rsy):
    g, me = lax.axis_index("dp"), lax.axis_index("expert")
    pieces = Pieces(normed.shape[1], n)
    mine, relays = pieces.of(me)
    greet(g, me, d, n)

    def first(k):
        t = lax.rem(me + k, n)
        p, ok = pieces.of(t)
        return remote(normed.at[:, pieces.cols(p)], relay.at[me], s1.at[k], r1.at[me], (g, t)), ok

    def first_in(k):
        s = lax.rem(me + n - k, n)
        return remote(normed.at[:, pieces.cols(mine)], relay.at[s], s1.at[k], r1.at[s], (g, s))

    def stat(k):
        t = lax.rem(me + k, n)
        return remote(stats, st_in.at[me], ss.at[k], rs.at[me], (g, t))

    def stat_in(k):
        s = lax.rem(me + n - k, n)
        return remote(stats, st_in.at[s], ss.at[k], rs.at[s], (g, s))

    for k in range(1, n):
        copy, ok = first(k)
        pl.when(ok)(copy.start)
    for k in range(1, n):
        stat(k).start()
    st_in[me] = stats[...]

    @pl.when(relays)
    def _():
        relay[me] = normed[:, pieces.cols(mine)]
        for k in range(1, n):
            first_in(k).wait_recv()
        for k in range(1, n):
            j = lax.rem(me + k, n)
            outbox[j] = relay[source[j]]
            remote(outbox.at[j], x.at[g, :, pieces.cols(mine)], s2.at[k], r2.at[mine], (g, j)).start()
        x[g, :, pieces.cols(mine)] = relay[source[me]]

    def along(p, c):
        here = x.at[g, :, pieces.cols(p)]
        return remote(here, here, sy.at[c, p], ry.at[g, p], (lax.rem(g + c, d), me))

    for k in range(n):
        i = lax.rem(me + n - k, n)
        p, ok = pieces.of(i)

        @pl.when(ok)
        def _():
            if k:
                remote(outbox.at[i], x.at[g, :, pieces.cols(p)], s2.at[k], r2.at[p], (g, i)).wait_recv()
            for c in range(1, d):
                along(p, c).start()

    for k in range(1, n):
        stat_in(k).wait_recv()
    mid = st_in[0]
    for s in range(1, n):
        mid = mid + st_in[s]
    st_mid[...] = mid
    st_dp[g] = mid
    for c in range(1, d):
        remote(st_mid, st_dp.at[g], ssy.at[c], rsy.at[g], (lax.rem(g + c, d), me)).start()
    for c in range(1, d):
        f = lax.rem(g + d - c, d)
        remote(st_mid, st_dp.at[f], ssy.at[c], rsy.at[f], (f, me)).wait_recv()
    total = st_dp[0]
    for f in range(1, d):
        total = total + st_dp[f]
    totals[...] = total

    for c in range(1, d):
        f = lax.rem(g + d - c, d)
        for p in range(pieces.count):
            there = x.at[f, :, pieces.cols(p)]
            remote(there, there, sy.at[c, p], ry.at[f, p], (f, me)).wait_recv()

    for k in range(1, n):
        copy, ok = first(k)
        pl.when(ok)(copy.wait_send)
        stat(k).wait_send()
    for c in range(1, d):
        remote(st_mid, st_dp.at[g], ssy.at[c], rsy.at[g], (lax.rem(g + c, d), me)).wait_send()
        for p in range(pieces.count):
            along(p, c).wait_send()

    @pl.when(relays)
    def _():
        for k in range(1, n):
            j = lax.rem(me + k, n)
            remote(outbox.at[j], x.at[g, :, pieces.cols(mine)], s2.at[k], r2.at[mine], (g, j)).wait_send()


def forward(normed, stats, source, d, n):
    rows, width = normed.shape
    pieces = Pieces(width, n)
    dma = pltpu.SemaphoreType.DMA
    return pl.pallas_call(
        functools.partial(forward_kernel, d, n),
        out_shape=(
            jax.ShapeDtypeStruct((d, rows, width), jnp.bfloat16),
            jax.ShapeDtypeStruct(stats.shape, jnp.float32),
        ),
        in_specs=[SMEM, VMEM, VMEM],
        out_specs=(VMEM, VMEM),
        scratch_shapes=[
            pltpu.VMEM((n, rows, pieces.w), jnp.bfloat16),
            pltpu.VMEM((n, rows, pieces.w), jnp.bfloat16),
            pltpu.VMEM((n,) + stats.shape, jnp.float32),
            pltpu.VMEM(stats.shape, jnp.float32),
            pltpu.VMEM((d,) + stats.shape, jnp.float32),
            dma((n,)), dma((n,)), dma((n,)), dma((pieces.count,)),
            dma((d, pieces.count)), dma((d, pieces.count)),
            dma((n,)), dma((n,)), dma((d,)), dma((d,)),
        ],
        compiler_params=pltpu.CompilerParams(
            collective_id=0, has_side_effects=True, vmem_limit_bytes=16 << 20
        ),
        cost_estimate=pl.CostEstimate(flops=10**6, bytes_accessed=100 << 20, transcendentals=0),
    )(source, normed, stats)


def back_kernel(d, n, source, partial, out, arrived, summed, relay, outbox, sy, ry, s1, r1, s2, r2):
    g, me = lax.axis_index("dp"), lax.axis_index("expert")
    pieces = Pieces(out.shape[1], n)
    mine, relays = pieces.of(me)
    greet(g, me, d, n)

    def along(p, c):
        t = lax.rem(g + c, d)
        return remote(partial.at[t, :, pieces.cols(p)], arrived.at[g, p], sy.at[c, p], ry.at[g, p], (t, me))

    def first(p, k, t):
        return remote(summed.at[p], relay.at[me], s1.at[k], r1.at[me], (g, t))

    order = [(k, lax.rem(me + k, n)) for k in range(n)]
    for k, t in order:
        p, ok = pieces.of(t)

        @pl.when(ok)
        def _():
            for c in range(1, d):
                along(p, c).start()

    for k, t in order:
        p, ok = pieces.of(t)

        @pl.when(ok)
        def _():
            for c in range(1, d):
                f = lax.rem(g + d - c, d)
                remote(partial.at[f, :, pieces.cols(p)], arrived.at[f, p], sy.at[c, p], ry.at[f, p], (f, me)).wait_recv()
            arrived[g, p] = partial[g, :, pieces.cols(p)]
            total = arrived[0, p].astype(jnp.float32)
            for f in range(1, d):
                total = total + arrived[f, p].astype(jnp.float32)
            summed[p] = total.astype(jnp.bfloat16)
            if k:
                first(p, k, t).start()
            else:
                relay[me] = total.astype(jnp.bfloat16)

    @pl.when(relays)
    def _():
        for k in range(1, n):
            s = lax.rem(me + n - k, n)
            remote(summed.at[mine], relay.at[s], s1.at[k], r1.at[s], (g, s)).wait_recv()
        for k in range(1, n):
            j = lax.rem(me + k, n)
            outbox[j] = relay[source[j]]
            remote(outbox.at[j], out.at[:, pieces.cols(mine)], s2.at[k], r2.at[mine], (g, j)).start()
        out[:, pieces.cols(mine)] = relay[source[me]]

    for k in range(1, n):
        i = lax.rem(me + n - k, n)
        p, ok = pieces.of(i)

        @pl.when(ok)
        def _():
            remote(outbox.at[i], out.at[:, pieces.cols(p)], s2.at[k], r2.at[p], (g, i)).wait_recv()

    for k, t in order:
        p, ok = pieces.of(t)

        @pl.when(ok)
        def _():
            for c in range(1, d):
                along(p, c).wait_send()
            if k:
                first(p, k, t).wait_send()

    @pl.when(relays)
    def _():
        for k in range(1, n):
            j = lax.rem(me + k, n)
            remote(outbox.at[j], out.at[:, pieces.cols(mine)], s2.at[k], r2.at[mine], (g, j)).wait_send()


def back(partial, source, n):
    d, rows, width = partial.shape
    pieces = Pieces(width, n)
    dma = pltpu.SemaphoreType.DMA
    return pl.pallas_call(
        functools.partial(back_kernel, d, n),
        out_shape=jax.ShapeDtypeStruct((rows, width), jnp.bfloat16),
        in_specs=[SMEM, VMEM],
        out_specs=VMEM,
        scratch_shapes=[
            pltpu.VMEM((d, pieces.count, rows, pieces.w), jnp.bfloat16),
            pltpu.VMEM((pieces.count, rows, pieces.w), jnp.bfloat16),
            pltpu.VMEM((n, rows, pieces.w), jnp.bfloat16),
            pltpu.VMEM((n, rows, pieces.w), jnp.bfloat16),
            dma((d, pieces.count)), dma((d, pieces.count)),
            dma((n,)), dma((n,)), dma((n,)), dma((pieces.count,)),
        ],
        compiler_params=pltpu.CompilerParams(
            collective_id=1, has_side_effects=True, vmem_limit_bytes=24 << 20
        ),
        cost_estimate=pl.CostEstimate(flops=10**6, bytes_accessed=100 << 20, transcendentals=0),
    )(source, partial)


def on_device(
    routed,
    expert_ids,
    norm_gain,
    gate_weight,
    up_weight,
    down_weight,
    old_place,
    new_place,
    probe_ids,
):
    n, d = lax.axis_size("expert"), lax.axis_size("dp")
    experts = EXP_DEV * n
    tokens = routed.shape[0] * d * n
    normed, stats = prepare(routed, expert_ids, probe_ids, norm_gain, experts)
    slot_index = jnp.arange(n, dtype=jnp.int32)
    matches = new_place[:, None] == old_place[None, :]
    sources = jnp.sum(jnp.where(matches, slot_index[None, :], 0), axis=1)
    targets = jnp.sum(jnp.where(matches, slot_index[:, None], 0), axis=0)
    x, totals = forward(normed, stats, targets, d, n)
    owned = lax.dynamic_slice_in_dim(totals, lax.axis_index("expert") * EXP_DEV, EXP_DEV, 1)
    expert_load = owned[0] * experts / (tokens * expert_ids.shape[1])
    expert_energy = owned[1] / owned[0]
    rows, width = normed.shape
    x = x.reshape(d * rows, width)
    gate_value = jnp.dot(x, gate_weight[0], preferred_element_type=jnp.float32)
    up_value = jnp.dot(x, up_weight[0], preferred_element_type=jnp.float32)
    hidden = (jax.nn.silu(gate_value) * up_value).astype(jnp.bfloat16)
    partial = jnp.dot(hidden, down_weight[0], preferred_element_type=jnp.float32)
    partial = partial.astype(jnp.bfloat16).reshape(d, rows, width)
    probe_out = back(partial, sources, n)
    return (expert_load, expert_energy, probe_out)


def solution(mesh):
    in_specs = (
        P(("dp", "expert"), None),
        P(("dp", "expert"), None),
        P(),
        P("expert", None, "dp"),
        P("expert", None, "dp"),
        P("expert", "dp", None),
        P(),
        P(),
        P(("dp", "expert")),
    )
    out_specs = (P("expert"), P("expert"), P(("dp", "expert"), None))
    return jax.shard_map(
        on_device, mesh=mesh, in_specs=in_specs, out_specs=out_specs, check_vma=False
    )
```

time: 211 us -> 111 us (0.53); the launches traced: 207 us -> 111 us
  Pallas kernels: 0 us -> 81.6 us
  waiting for transfers between devices: 72.6 us -> 0 us
  blocking collectives: 57.7 us -> 0 us
  starting transfers between devices: 18.6 us -> 0 us
  between operations: 14.2 us -> 0.67 us
  local copies, waits for them, and re-layouts: 14.3 us -> 4.64 us
  other arithmetic: 5.49 us -> 1.39 us
    pallas_call x0 -> x3, Pallas kernels: none -> 81.6 us  [the longest x1 42.4 us: forward(): pl.pallas_call(functools.partial(forward_kernel, d, n), out_shape=(jax.Sh...]
    psum x1 -> x0, blocking collectives: 38 us -> none  [on_device(): totals = lax.psum(local_stats, ('dp', 'expert'))]
    all_to_all x3 -> x0, waiting for transfers between devices: 27.9 us -> none  [the longest x2 27.9 us: relay_rows(): lax.all_to_all(shaped, 'expert', split_axis=0, concat_axis=0, tiled=True)]
    all_gather x1 -> x0, waiting for transfers between devices: 23 us -> none  [expert_block(): piece = lax.all_gather(normed, 'dp', axis=0, tiled=True)]
    reduce_scatter x1 -> x0, waiting for transfers between devices: 21.6 us -> none  [expert_block(): lax.psum_scatter(partial_sums.astype(jnp.bfloat16), 'dp', scatter_dimensi...]
    all_to_all x1 -> x0, blocking collectives: 19.8 us -> none  [relay_rows(): lax.all_to_all(jnp.take(lax.all_to_all(shaped, 'expert', split_axis=0, co...]
    all_to_all x3 -> x0, starting transfers between devices: 18.5 us -> none  [the longest x2 12.8 us: relay_rows(): lax.all_to_all(shaped, 'expert', split_axis=0, concat_axis=0, tiled=True)]
    gather x5 -> x0, local copies, waits for them, and re-layouts: 5.65 us -> none  [the longest x2 3.55 us: on_device(): picked_rows = jnp.take(routed, probe_ids, axis=0).astype(jnp.float32)]
  transfers between devices with their start and end apart: 5 -> 0, of which waited for: 4 -> 0; matrix products, arithmetic and copies ran while one was open for 1% -> 0% of each run, Pallas kernels for 0% -> 0%
where the time goes in v1:
time: 111 us
  Pallas kernels  81.6 us (74%)
  matrix products  22.5 us (20%)
  local copies, waits for them, and re-layouts  4.64 us (4%)
  other arithmetic  1.39 us (1%)
    pallas_call x1, Pallas kernels, forward(): pl.pallas_call(functools.partial(forward_kernel, d, n), out_shape=(jax.Sh...  42.4 us
    pallas_call x1, Pallas kernels, back(): pl.pallas_call(functools.partial(back_kernel, d, n), out_shape=jax.ShapeD...  38.5 us
    dot_general x1, matrix products, on_device(): jnp.dot(hidden, down_weight[0], preferred_element_type=jnp.float32)  14.6 us
    dot_general x1, matrix products, on_device(): gate_value = jnp.dot(x, gate_weight[0], preferred_element_type=jnp.float32)  7.86 us
    unnamed x4, local copies, waits for them, and re-layouts  3.1 us

profile of v1, /device:TPU:27, one launch (start us, length us, event | category | flops | bytes accessed | tf_op | source)
XLA Modules:
  0.0 110.8 jit_solution(11230837408538317914)
XLA Ops:
  0.6 0.9 fusion.24
  1.5 0.7 copy.15.probe
  2.2 0.7 reshape.24.gain
  3.0 0.8 copy.14.ids
  3.8 0.0 copy-start
  3.8 1.5 %copy-done = bf16[128,7168]{1,0:T(8,128)(2,1)S(1)} copy-done((bf16[128,7168]{1,0:T(8,128)(2,1)S(1)}, bf16[128,7168]{1,0:T(8,128)(2,1)}, u32[]{:S(2)}) %copy-start) | copy-done | bytes 1835032
  5.3 0.7 shard_map.112
  6.0 42.4 %shard_map.113 = (bf16[2,40,7168]{2,1,0:T(8,128)(2,1)S(1)}, f32[8,128]{1,0:T(8,128)S(1)}) custom-call(s32[16]{0:T(128)S(1)} %get-tuple-element.12.source, bf16[40,7168]{1,0:T(8,128)(2,1)S(1)} %get-tuple-element.7.normed, f32[8,128]{1,0:T(8,128)S(1)} %get-tuple-element.8.stats), custom_call_target="tpu_custom_call" | custom-call | flops 1000000 | bytes 104857600 | tf_op jit(solution)/shard_map/pallas_call | solution.py:199
  48.4 0.1 constant_dynamic-slice_fusion
  48.5 0.5 fusion.25
  49.0 7.9 %fusion.4 = f32[80,1024]{1,0:T(8,128)S(1)} fusion(bf16[80,7168]{1,0:T(8,128)(2,1)S(1)} %bitcast.26, bf16[1,7168,1024]{2,1,0:T(8,128)(2,1)} %param.12), kind=kOutput, calls=%fused_computation.4 | convolution fusion | flops 1174405120 | bytes 16154624 | tf_op jit(solution)/shard_map/dot_general | solution.py:349
  56.9 14.6 %fusion.6 = bf16[80,7168]{1,0:T(8,128)(2,1)S(1)} fusion(bf16[1,1024,7168]{2,1,0:T(8,128)(2,1)} %param.14, bf16[80,7168]{1,0:T(8,128)(2,1)S(1)} %bitcast.27, bf16[1,7168,1024]{2,1,0:T(8,128)(2,1)} %param.13, f32[80,1024]{1,0:T(8,128)S(1)} %fusion.4), kind=kOutput, calls=%fused_computation.6 | convolution fusion | flops 2349875200 | bytes 31981568 | tf_op jit(solution)/shard_map/dot_general | solution.py:352
  71.5 38.5 %shard_map.114 = bf16[40,7168]{1,0:T(8,128)(2,1)S(1)} custom-call(s32[16]{0:T(128)S(1)} %get-tuple-element.11.source, bf16[2,40,7168]{2,1,0:T(8,128)(2,1)S(1)} %bitcast.28), custom_call_target="tpu_custom_call" | custom-call | flops 1000000 | bytes 104857600 | tf_op jit(solution)/shard_map/pallas_call | solution.py:304
  110.0 0.8 copy.17
Async XLA Ops:
  3.8 1.5 %copy-start = (bf16[128,7168]{1,0:T(8,128)(2,1)S(1)}, bf16[128,7168]{1,0:T(8,128)(2,1)}, u32[]{:S(2)}) copy-start(bf16[128,7168]{1,0:T(8,128)(2,1)} %routed.1) | copy-start | bytes 5505028

commit v2 on v1

v2 whole, which is shorter than its diff:
```python
import functools

import jax
import jax.numpy as jnp
from jax import lax
from jax.experimental import pallas as pl
from jax.experimental.pallas import tpu as pltpu
from jax.sharding import PartitionSpec as P

EXP_DEV = 8
LANES = 128
MESH = pl.DeviceIdType.MESH
VMEM = pl.BlockSpec(memory_space=pltpu.VMEM)
SMEM = pl.BlockSpec(memory_space=pltpu.SMEM)
epsilon = 1e-06


def piece_width(width, n):
    w = LANES * -(-width // (LANES * n))
    while width % w:
        w += LANES
    return w


def prepare_kernel(routed, ids, probe, gain, normed, stats):
    tokens, width = routed.shape
    experts = stats.shape[1]
    total = jnp.zeros((tokens, LANES), jnp.float32)
    for c in range(width // LANES):
        x = routed[:, c * LANES : (c + 1) * LANES].astype(jnp.float32)
        total = total + x * x
    mean_square = jnp.sum(total, axis=1, keepdims=True) / width
    lane = lax.broadcasted_iota(jnp.int32, (tokens, experts), 1)
    chosen = jnp.zeros((tokens, experts), jnp.float32)
    for k in range(ids.shape[1]):
        chosen = chosen + jnp.where(ids[:, k : k + 1] == lane, 1.0, 0.0)
    stats[...] = jnp.zeros_like(stats)
    stats[0:1, :] = jnp.sum(chosen, axis=0, keepdims=True)
    stats[1:2, :] = jnp.sum(chosen * mean_square, axis=0, keepdims=True)
    probes = probe.shape[0]
    row = lax.broadcasted_iota(jnp.int32, (tokens, tokens), 0)
    column = lax.broadcasted_iota(jnp.int32, (tokens, tokens), 1)
    flat = jnp.sum(jnp.where(row == column, mean_square, 0.0), axis=0, keepdims=True)
    pick = probe[...] == lax.broadcasted_iota(jnp.int32, (probes, tokens), 1)
    scale = lax.rsqrt(jnp.sum(jnp.where(pick, flat, 0.0), axis=1, keepdims=True) + epsilon)
    pick = jnp.where(pick, 1.0, 0.0).astype(jnp.bfloat16)
    step = 512 if width % 512 == 0 else LANES
    for c in range(width // step):
        cols = slice(c * step, (c + 1) * step)
        rows = jnp.dot(pick, routed[:, cols], preferred_element_type=jnp.float32)
        normed[:, cols] = (rows * scale * gain[:, cols].astype(jnp.float32)).astype(jnp.bfloat16)


def prepare(routed, expert_ids, probe_ids, norm_gain, experts):
    probes = probe_ids.shape[0]
    width = routed.shape[1]
    return pl.pallas_call(
        prepare_kernel,
        out_shape=(
            jax.ShapeDtypeStruct((probes, width), jnp.bfloat16),
            jax.ShapeDtypeStruct((8, experts), jnp.float32),
        ),
        in_specs=[VMEM] * 4,
        out_specs=(VMEM, VMEM),
        compiler_params=pltpu.CompilerParams(vmem_limit_bytes=16 << 20),
        cost_estimate=pl.CostEstimate(flops=10**8, bytes_accessed=3 << 20, transcendentals=0),
    )(routed, expert_ids, probe_ids.reshape(probes, 1), norm_gain.reshape(1, width))


def remote(src, dst, send, recv, device):
    return pltpu.make_async_remote_copy(
        src_ref=src, dst_ref=dst, send_sem=send, recv_sem=recv, device_id=device, device_id_type=MESH
    )


def greet(g, me, d, n):
    barrier = pltpu.get_barrier_semaphore()
    for k in range(1, n):
        pl.semaphore_signal(barrier, inc=1, device_id=(g, lax.rem(me + k, n)), device_id_type=MESH)
    for c in range(1, d):
        pl.semaphore_signal(barrier, inc=1, device_id=(lax.rem(g + c, d), me), device_id_type=MESH)
    pl.semaphore_wait(barrier, n - 1 + d - 1)


class Pieces:
    def __init__(self, width, n):
        self.n = n
        self.w = piece_width(width, n)
        self.count = width // self.w

    def of(self, i):
        p = (i * self.count + self.n - 1) // self.n
        return jnp.minimum(p, self.count - 1), (p < self.count) & ((p * self.n) // self.count == i)

    def cols(self, p):
        return pl.ds(pl.multiple_of(p * self.w, self.w), self.w)


def fused_kernel(d, n, lag, source, home, normed, stats, gate_hbm, up_hbm, down_hbm, out, totals,
                 wg, wu, wd, x, gate_sum, up_sum, hidden, partial, arrived, summed, relay, outbox, relay2, outbox2,
                 st_in, st_mid, st_dp, sw, sd, s1, r1, s2, r2, sy, ry, ss, rs, ssy, rsy, s3, r3, s4, r4, sz, rz):
    g, me = lax.axis_index("dp"), lax.axis_index("expert")
    rows, width = normed.shape
    pieces = Pieces(width, n)
    mine, relays = pieces.of(me)
    count = pieces.count
    tall = d * rows
    down_step = wd.shape[0] // sd.shape[0]

    loads = []
    for p in range(count):
        part = pl.ds(p * pieces.w, pieces.w)
        loads.append(pltpu.make_async_copy(gate_hbm.at[part, :], wg.at[part, :], sw.at[0, p]))
        loads.append(pltpu.make_async_copy(up_hbm.at[part, :], wu.at[part, :], sw.at[1, p]))
    for p in range(sd.shape[0]):
        part = pl.ds(p * down_step, down_step)
        loads.append(pltpu.make_async_copy(down_hbm.at[part, :], wd.at[part, :], sd.at[p]))
    for load in loads:
        load.start()
    greet(g, me, d, n)

    def first(k):
        t = lax.rem(me + k, n)
        p, ok = pieces.of(t)
        return remote(normed.at[:, pieces.cols(p)], relay.at[me], s1.at[k], r1.at[me], (g, t)), ok

    def first_in(k):
        s = lax.rem(me + n - k, n)
        return remote(normed.at[:, pieces.cols(mine)], relay.at[s], s1.at[k], r1.at[s], (g, s))

    def stat(k):
        t = lax.rem(me + k, n)
        return remote(stats, st_in.at[me], ss.at[k], rs.at[me], (g, t))

    def stat_in(k):
        s = lax.rem(me + n - k, n)
        return remote(stats, st_in.at[s], ss.at[k], rs.at[s], (g, s))

    def second(k):
        j = lax.rem(me + k, n)
        return remote(outbox.at[j], x.at[g, :, pieces.cols(mine)], s2.at[k], r2.at[mine], (g, j))

    def along(p, c):
        here = x.at[g, :, pieces.cols(p)]
        return remote(here, here, sy.at[c, p], ry.at[g, p], (lax.rem(g + c, d), me))

    for k in range(1, n):
        copy, ok = first(k)
        pl.when(ok)(copy.start)
    for k in range(1, n):
        stat(k).start()
    st_in[me] = stats[...]
    gate_sum[...] = jnp.zeros_like(gate_sum)
    up_sum[...] = jnp.zeros_like(up_sum)

    @pl.when(relays)
    def _():
        relay[me] = normed[:, pieces.cols(mine)]
        for k in range(1, n):
            first_in(k).wait_recv()
        for k in range(1, n):
            j = lax.rem(me + k, n)
            outbox[j] = relay[source[j]]
            second(k).start()
        x[g, :, pieces.cols(mine)] = relay[source[me]]

    for load in loads:
        load.wait()

    def take(k):
        i = lax.rem(me + n - k, n)
        p, ok = pieces.of(i)

        @pl.when(ok)
        def _():
            @pl.when(k > 0)
            def _():
                remote(outbox.at[i], x.at[g, :, pieces.cols(p)], s2.at[k], r2.at[p], (g, i)).wait_recv()
            for c in range(1, d):
                along(p, c).start()

    def absorb(k):
        p, ok = pieces.of(lax.rem(me + n - k, n))

        @pl.when(ok)
        def _():
            for c in range(1, d):
                f = lax.rem(g + d - c, d)
                there = x.at[f, :, pieces.cols(p)]
                remote(there, there, sy.at[c, p], ry.at[f, p], (f, me)).wait_recv()
            part = x[:, :, pieces.cols(p)].astype(jnp.float32).reshape(tall, pieces.w).astype(jnp.bfloat16)
            gate_sum[...] += jnp.dot(part, wg[pieces.cols(p), :], preferred_element_type=jnp.float32)
            up_sum[...] += jnp.dot(part, wu[pieces.cols(p), :], preferred_element_type=jnp.float32)

    for k in range(lag):
        take(k)

    @pl.loop(lag, n)
    def _(k):
        take(k)
        absorb(k - lag)

    @pl.loop(n - lag, n)
    def _(k):
        absorb(k)

    gate = gate_sum[...]
    hidden[...] = (gate / (1.0 + jnp.exp(-gate)) * up_sum[...]).astype(jnp.bfloat16)

    def home_copy(p, c):
        t = lax.rem(g + c, d)
        return remote(partial.at[p, t], arrived.at[g, p], sz.at[c, p], rz.at[g, p], (t, me))

    def third(p, k, t):
        return remote(summed.at[p], relay2.at[me], s3.at[k], r3.at[me], (g, t))

    def fourth(k):
        j = lax.rem(me + k, n)
        return remote(outbox2.at[j], out.at[:, pieces.cols(mine)], s4.at[k], r4.at[mine], (g, j))

    def make(k):
        p, ok = pieces.of(lax.rem(me + k, n))

        @pl.when(ok)
        def _():
            value = jnp.dot(hidden[...], wd[:, pieces.cols(p)], preferred_element_type=jnp.float32)
            partial[p] = value.reshape(d, rows, pieces.w).astype(jnp.bfloat16)
            for c in range(1, d):
                home_copy(p, c).start()

    def add(k):
        t = lax.rem(me + k, n)
        p, ok = pieces.of(t)

        @pl.when(ok)
        def _():
            for c in range(1, d):
                f = lax.rem(g + d - c, d)
                remote(partial.at[p, f], arrived.at[f, p], sz.at[c, p], rz.at[f, p], (f, me)).wait_recv()
            arrived[g, p] = partial[p, g]
            total = arrived[0, p].astype(jnp.float32)
            for f in range(1, d):
                total = total + arrived[f, p].astype(jnp.float32)

            @pl.when(t != me)
            def _():
                summed[p] = total.astype(jnp.bfloat16)
                third(p, k, t).start()

            @pl.when(t == me)
            def _():
                relay2[me] = total.astype(jnp.bfloat16)

    @pl.loop(1, lag + 1)
    def _(k):
        make(k)

    @pl.loop(lag + 1, n + 1)
    def _(k):
        make(k)
        add(k - lag)

    @pl.loop(n + 1 - lag, n + 1)
    def _(k):
        add(k)

    for k in range(1, n):
        stat_in(k).wait_recv()
    mid = st_in[0]
    for s in range(1, n):
        mid = mid + st_in[s]
    st_mid[...] = mid
    st_dp[g] = mid
    for c in range(1, d):
        remote(st_mid, st_dp.at[g], ssy.at[c], rsy.at[g], (lax.rem(g + c, d), me)).start()

    @pl.when(relays)
    def _():
        for k in range(1, n):
            s = lax.rem(me + n - k, n)
            remote(summed.at[mine], relay2.at[s], s3.at[k], r3.at[s], (g, s)).wait_recv()
        for k in range(1, n):
            j = lax.rem(me + k, n)
            outbox2[j] = relay2[home[j]]
            fourth(k).start()
        out[:, pieces.cols(mine)] = relay2[home[me]]

    for c in range(1, d):
        f = lax.rem(g + d - c, d)
        remote(st_mid, st_dp.at[f], ssy.at[c], rsy.at[f], (f, me)).wait_recv()
    total = st_dp[0]
    for f in range(1, d):
        total = total + st_dp[f]
    totals[...] = total

    for k in range(1, n):
        copy, ok = first(k)
        pl.when(ok)(copy.wait_send)
        stat(k).wait_send()
    for c in range(1, d):
        remote(st_mid, st_dp.at[g], ssy.at[c], rsy.at[g], (lax.rem(g + c, d), me)).wait_send()
        for p in range(count):
            along(p, c).wait_send()
            home_copy(p, c).wait_send()
    for k in range(1, n):
        t = lax.rem(me + k, n)
        p, ok = pieces.of(t)
        pl.when(ok)(third(p, k, t).wait_send)

    @pl.when(relays)
    def _():
        for k in range(1, n):
            second(k).wait_send()
            fourth(k).wait_send()

    for k in range(1, n):
        i = lax.rem(me + n - k, n)
        p, ok = pieces.of(i)

        @pl.when(ok)
        def _():
            remote(outbox2.at[i], out.at[:, pieces.cols(p)], s4.at[k], r4.at[p], (g, i)).wait_recv()


def fused(normed, stats, source, home, gate, up, down, d, n):
    rows, width = normed.shape
    pieces = Pieces(width, n)
    units = gate.shape[1]
    count, w = pieces.count, pieces.w
    dma = pltpu.SemaphoreType.DMA
    block = lambda *shape: pltpu.VMEM(shape, jnp.bfloat16)
    wide = lambda *shape: pltpu.VMEM(shape, jnp.float32)
    anywhere = pl.BlockSpec(memory_space=pltpu.HBM)
    return pl.pallas_call(
        functools.partial(fused_kernel, d, n, 4),
        out_shape=(
            jax.ShapeDtypeStruct((rows, width), jnp.bfloat16),
            jax.ShapeDtypeStruct(stats.shape, jnp.float32),
        ),
        in_specs=[SMEM, SMEM, VMEM, VMEM, anywhere, anywhere, anywhere],
        out_specs=(VMEM, VMEM),
        scratch_shapes=[
            block(width, units), block(width, units), block(units, width),
            block(d, rows, width),
            wide(d * rows, units), wide(d * rows, units), block(d * rows, units),
            block(count, d, rows, w), block(d, count, rows, w), block(count, rows, w),
            block(n, rows, w), block(n, rows, w), block(n, rows, w), block(n, rows, w),
            wide(n, *stats.shape), wide(*stats.shape), wide(d, *stats.shape),
            dma((2, count)), dma((8,)),
            dma((n,)), dma((n,)), dma((n,)), dma((count,)), dma((d, count)), dma((d, count)),
            dma((n,)), dma((n,)), dma((d,)), dma((d,)),
            dma((n,)), dma((n,)), dma((n,)), dma((count,)), dma((d, count)), dma((d, count)),
        ],
        compiler_params=pltpu.CompilerParams(
            collective_id=0, has_side_effects=True, vmem_limit_bytes=62 << 20
        ),
    )(source, home, normed, stats, gate, up, down)


def on_device(
    routed,
    expert_ids,
    norm_gain,
    gate_weight,
    up_weight,
    down_weight,
    old_place,
    new_place,
    probe_ids,
):
    n, d = lax.axis_size("expert"), lax.axis_size("dp")
    experts = EXP_DEV * n
    tokens = routed.shape[0] * d * n
    normed, stats = prepare(routed, expert_ids, probe_ids, norm_gain, experts)
    slot_index = jnp.arange(n, dtype=jnp.int32)
    matches = new_place[:, None] == old_place[None, :]
    sources = jnp.sum(jnp.where(matches, slot_index[None, :], 0), axis=1)
    targets = jnp.sum(jnp.where(matches, slot_index[:, None], 0), axis=0)
    probe_out, totals = fused(
        normed, stats, targets, sources, gate_weight[0], up_weight[0], down_weight[0], d, n
    )
    owned = lax.dynamic_slice_in_dim(totals, lax.axis_index("expert") * EXP_DEV, EXP_DEV, 1)
    expert_load = owned[0] * experts / (tokens * expert_ids.shape[1])
    expert_energy = owned[1] / owned[0]
    return (expert_load, expert_energy, probe_out)


def solution(mesh):
    in_specs = (
        P(("dp", "expert"), None),
        P(("dp", "expert"), None),
        P(),
        P("expert", None, "dp"),
        P("expert", None, "dp"),
        P("expert", "dp", None),
        P(),
        P(),
        P(("dp", "expert")),
    )
    out_specs = (P("expert"), P("expert"), P(("dp", "expert"), None))
    return jax.shard_map(
        on_device, mesh=mesh, in_specs=in_specs, out_specs=out_specs, check_vma=False
    )
```

time: 111 us -> 92.1 us (0.83)
  matrix products: 22.5 us -> 0 us
  local copies, waits for them, and re-layouts: 4.64 us -> 7.79 us
    dot_general x2 -> x0, matrix products: 22.5 us -> none  [the longest x1 14.6 us: on_device(): jnp.dot(hidden, down_weight[0], preferred_element_type=jnp.float32)]
    unnamed x4 -> x8, local copies, waits for them, and re-layouts: 3.1 us -> 5.58 us
    pallas_call x2 -> x1, Pallas kernels: 80.9 us -> 80.6 us  [fused(): pl.pallas_call(functools.partial(fused_kernel, d, n, 4), out_shape=(jax.S...]
where the time goes in v2:
time: 92.1 us; the launch traced here: 91.7 us
  Pallas kernels  81.4 us (88%)
  local copies, waits for them, and re-layouts  7.79 us (8%)
  other arithmetic  1.9 us (2%)
    pallas_call x1, Pallas kernels, fused(): pl.pallas_call(functools.partial(fused_kernel, d, n, 4), out_shape=(jax.S...  80.6 us
    unnamed x8, local copies, waits for them, and re-layouts  5.58 us

profile of v2, /device:TPU:27, one launch (start us, length us, event | category | flops | bytes accessed | tf_op | source)
XLA Modules:
  0.0 91.7 jit_solution(3017130459741557474)
XLA Ops:
  0.6 1.4 %fusion.1 = (s32[16]{0:T(128)}, s32[16]{0:T(128)}) fusion(s32[16]{0:T(128)} %param.15, s32[16]{0:T(128)} %param.16), kind=kLoop, calls=%fused_computation.3 | loop fusion | flops 1248 | bytes 256 | tf_op jit(solution)/shard_map/reduce_sum | solution.py:377
  2.0 0.8 copy.14.ids
  2.8 0.7 copy.15.probe
  3.5 0.7 reshape.18.gain
  4.3 0.0 copy-start
  4.3 1.5 %copy-done = bf16[128,7168]{1,0:T(8,128)(2,1)S(1)} copy-done((bf16[128,7168]{1,0:T(8,128)(2,1)S(1)}, bf16[128,7168]{1,0:T(8,128)(2,1)}, u32[]{:S(2)}) %copy-start) | copy-done | bytes 1835032
  5.8 0.7 shard_map.112
  6.5 0.0 copy-start.1
  6.5 0.8 copy-done.1
  7.3 0.0 copy-start.2
  7.3 0.6 copy-done.2
  7.9 80.6 %shard_map.113 = (bf16[40,7168]{1,0:T(8,128)(2,1)}, f32[8,128]{1,0:T(8,128)}) custom-call(s32[16]{0:T(128)} %get-tuple-element.12.source, s32[16]{0:T(128)} %get-tuple-element.11.home, bf16[40,7168]{1,0:T(8,128)(2,1)} %copy-done.1, f32[8,128]{1,0:T(8,128)} %copy-done.2, bf16[7168,1024]{1,0:T(8,128)(2,1)} %bitcast.8, bf16[7168,1024]{1,0:T(8,128)(2,1)} %bitcast.9, ...), custom_call_target="tpu_custom_call" | custom-call | tf_op jit(solution)/shard_map/pallas_call | solution.py:334
  88.6 0.7 constant_dynamic-slice_fusion
  89.3 0.5 fusion.2
  89.8 1.9 %copy.17 = bf16[40,7168]{1,0:T(8,128)(2,1)} copy(bf16[40,7168]{1,0:T(8,128)(2,1)} %get-tuple-element.20) | data formatting | bytes 1146880
Async XLA Ops:
  4.3 1.5 %copy-start = (bf16[128,7168]{1,0:T(8,128)(2,1)S(1)}, bf16[128,7168]{1,0:T(8,128)(2,1)}, u32[]{:S(2)}) copy-start(bf16[128,7168]{1,0:T(8,128)(2,1)} %routed.1) | copy-start | bytes 5505028
  6.5 0.8 copy-start.1
  7.3 0.6 copy-start.2
